TPU v7x, 32 devices: a whole 2x2x4 slice. The times are simulated.
32 devices in a mesh: layer: 8 (over y, x, core), dp: 4 (over z).
Axes of the slice: x: 2, y: 2, z: 4, core: 2. Of those that a mesh axis runs over, the one named last changes fastest.
Arguments:
- initial: float32 [256, 1024], P('dp'), may hold values from -6 to 6
- norm_gains: float32 [32, 1024], P('layer'), may hold values from 0.25 to 1.75
- first_weights: bfloat16 [32, 1024, 2048], P('layer'), may hold values from -0.1875 to 0.1875
- second_weights: bfloat16 [32, 2048, 1024], P('layer'), may hold values from -0.046875 to 0.046875
Outputs:
- layer_states: float32 [32, 256, 1024], P('layer', 'dp')
- residual_ratios: float32 [7], replicated
- coarse_defects_four: float32 [32, 256, 1024], P('layer', 'dp')
- coarse_defects_sixteen: float32 [32, 256, 1024], P('layer', 'dp')
All inputs are finite; a program needn't handle non-finite values.
Results may differ from a plain program's by a relative error of at most 0.02.
Values sent between devices are 32-bit elements; how exact they have to be, the bound alone decides.
A program may use at most 128 MiB of HBM per device.

v0:
```python
import jax
import jax.numpy as jnp
from jax import lax
from jax.experimental import pallas as pl
from jax.experimental.pallas import tpu as pltpu
from jax.sharding import PartitionSpec as P

epsilon = 1e-06


def shifted(block, axis, distance):
    devices = range(lax.axis_size(axis))
    route = [(i - distance, i) for i in devices if i - distance in devices]
    return lax.ppermute(block, axis, route)


def branch(row_block, weight_in, weight_out, gain_row):
    mean_square = jnp.mean(row_block * row_block, axis=-1, keepdims=True)
    normed = (row_block * lax.rsqrt(mean_square + epsilon) * gain_row).astype(jnp.bfloat16)
    hidden = jax.nn.gelu(
        jnp.dot(normed, weight_in, preferred_element_type=jnp.float32), approximate=True
    ).astype(jnp.bfloat16)
    return jnp.dot(hidden, weight_out, preferred_element_type=jnp.float32)


def local(initial, norm_gains, first_weights, second_weights):
    slot_count = first_weights.shape[0]
    sections = lax.axis_size("layer")
    layer_total = slot_count * sections
    norm_count = layer_total // 4 - 1
    first_point = lax.axis_index("layer") * slot_count
    points = first_point + jnp.arange(slot_count, dtype=jnp.int32) + 1
    spacings = (1, 4, 16)

    def shaped(flags, rank):
        return flags.reshape((slot_count,) + (1,) * (rank - 1))

    def previous(values, level_index):
        spacing = spacings[level_index]
        if spacing >= slot_count:
            portion = values
            distance = spacing // slot_count
        else:
            portion = values[slot_count - spacing :]
            distance = 1
        if level_index == 0:
            arrived = shifted(portion, "layer", distance)
        elif level_index == 1:
            arrived = shifted(portion, "layer", distance)
        else:
            arrived = shifted(portion, "layer", distance)
        if spacing < slot_count:
            arrived = jnp.concatenate([arrived, values[: slot_count - spacing]], axis=0)
        return arrived

    def incoming(values, level_index, anchor):
        arrived = previous(values, level_index)
        from_anchor = shaped(points - spacings[level_index] == 0, values.ndim)
        return jnp.where(from_anchor, anchor, arrived)

    def advance(before, level_index, active, right_side):
        factor = float(spacings[level_index])
        results = []
        for slot in range(slot_count):

            def advance_compute(values, source, slot=slot):
                return (
                    values
                    + factor
                    * branch(values, first_weights[slot], second_weights[slot], norm_gains[slot])
                    + source
                )

            def advance_unchanged(values, source):
                return values

            source = right_side[slot] if right_side is not None else jnp.zeros_like(before[slot])
            results.append(
                lax.cond(active[slot], advance_compute, advance_unchanged, before[slot], source)
            )
        return jnp.stack(results)

    def relaxation(current, level_index, residues, right_side, anchor):
        modulus = 4 * spacings[level_index]
        for residue in residues:
            before = incoming(current, level_index, anchor)
            active = points % modulus == residue
            current = jnp.where(
                shaped(active, 3), advance(before, level_index, active, right_side), current
            )
        return (current, None)

    def restrict(current, level_index, right_side, anchor):
        spacing = spacings[level_index]
        factor = float(spacing)
        wide_factor = float(4 * spacing)
        before = incoming(current, level_index, anchor)
        far_state = incoming(current, level_index + 1, anchor)
        active = points % (4 * spacing) == 0
        row_count = current.shape[1]
        coarse_list = []
        gap_list = []
        step_list = []
        for slot in range(slot_count):

            def restrict_compute(near, distant, held, source, slot=slot):
                update = branch(
                    jnp.concatenate([near, distant], axis=0),
                    first_weights[slot],
                    second_weights[slot],
                    norm_gains[slot],
                )
                near_term = update[:row_count]
                fine_value = near + factor * near_term + source
                coarse = fine_value - (distant + wide_factor * update[row_count:])
                gap = fine_value - held
                return (coarse, jnp.sum(gap * gap), jnp.sum(near_term * near_term))

            def restrict_unchanged(near, distant, held, source):
                nothing = jnp.zeros((), near.dtype)
                return (jnp.zeros_like(near), nothing, nothing)

            source = right_side[slot] if right_side is not None else jnp.zeros_like(before[slot])
            coarse, gap_sum, step_sum = lax.cond(
                active[slot],
                restrict_compute,
                restrict_unchanged,
                before[slot],
                far_state[slot],
                current[slot],
                source,
            )
            coarse_list.append(coarse)
            gap_list.append(gap_sum)
            step_list.append(step_sum)
        return (jnp.stack(coarse_list), jnp.stack(gap_list), jnp.stack(step_list))

    def defects(current, level_index, anchor):
        spacing = spacings[level_index]
        factor = float(spacing)
        before = incoming(current, level_index, anchor)
        stepped = []
        for slot in range(slot_count):
            stepped.append(
                before[slot]
                + factor
                * branch(before[slot], first_weights[slot], second_weights[slot], norm_gains[slot])
            )
        valid = shaped(points >= spacing, 3)
        return jnp.where(valid, current - jnp.stack(stepped), 0.0)

    def multigrid_cycle(anchor):
        current = jnp.broadcast_to(anchor, (slot_count,) + anchor.shape)
        current, unused = relaxation(current, 0, (1, 2, 3), None, anchor)
        current, unused = relaxation(current, 0, (0,), None, anchor)
        current, carried = relaxation(current, 0, (1, 2, 3), None, anchor)
        rhs_one, gap_sums, step_sums = restrict(current, 0, None, anchor)
        current, carried = relaxation(current, 1, (4, 8, 12), rhs_one, anchor)
        rhs_two, unused_gaps, unused_steps = restrict(current, 1, rhs_one, anchor)
        for coarse_step in range(1, layer_total // 16 + 1):
            active = points == 16 * coarse_step
            before = incoming(current, 2, anchor)
            current = jnp.where(shaped(active, 3), advance(before, 2, active, rhs_two), current)
        current, unused = relaxation(current, 1, (4, 8, 12), rhs_one, anchor)
        current, unused = relaxation(current, 0, (1, 2, 3), None, anchor)
        defects_four = defects(current, 1, anchor)
        defects_sixteen = defects(current, 2, anchor)
        return (current, gap_sums, step_sums, defects_four, defects_sixteen)

    portions = [initial]
    outcomes = [multigrid_cycle(portion) for portion in portions]
    layer_states = jnp.concatenate([outcome[0] for outcome in outcomes], axis=1)
    defects_four = jnp.concatenate([outcome[3] for outcome in outcomes], axis=1)
    defects_sixteen = jnp.concatenate([outcome[4] for outcome in outcomes], axis=1)
    gap_sums = outcomes[0][1]
    step_sums = outcomes[0][2]
    counted = (points % 4 == 0) & (points >= 8)
    entry_index = points // 4 - 2
    one_hot = (
        (jnp.arange(norm_count, dtype=jnp.int32)[None, :] == entry_index[:, None])
        & counted[:, None]
    ).astype(jnp.float32)
    gap_vector = jnp.sum(gap_sums[:, None] * one_hot, axis=0)
    step_vector = jnp.sum(step_sums[:, None] * one_hot, axis=0)
    gap_total, step_total = lax.psum((gap_vector, step_vector), ("layer", "dp"))
    residual_ratios = jnp.sqrt(gap_total / (step_total + epsilon))
    return (layer_states, residual_ratios, defects_four, defects_sixteen)


def coarse_kernel(
    sections, copies,
    initial, start, rhs_one, far_step, tile, gain, w_in, w_out,
    point, left, far, totals,
    cur, slots, ends, normed, total, across, along, summed,
    send, arrive, end_arrive, across_send, across_arrive, along_send, along_arrive,
):
    here = lax.axis_index("layer")
    depth = lax.axis_index("dp")
    blocks = sections // 4
    wide_end = blocks + 2
    rounds = wide_end + 2
    ff = w_in.shape[2]
    width = ff // 4

    def to(layer, dp):
        return dict(device_id=(layer, dp), device_id_type=pl.DeviceIdType.MESH)

    cur[...] = start[...]
    across[depth] = tile[...]

    barrier = pltpu.get_barrier_semaphore()
    for k in range(1, sections):
        pl.semaphore_signal(barrier, inc=1, **to(lax.rem(here + k, sections), depth))
    for k in range(1, copies):
        pl.semaphore_signal(barrier, inc=1, **to(here, lax.rem(depth + k, copies)))
    pl.semaphore_wait(barrier, sections + copies - 2)

    def across_copy(k):
        return pltpu.make_async_remote_copy(
            src_ref=tile, dst_ref=across.at[depth],
            send_sem=across_send.at[k - 1], recv_sem=across_arrive.at[k - 1],
            **to(here, lax.rem(depth + k, copies)),
        )

    for k in range(1, copies):
        across_copy(k).start()

    def wide(d, r):
        return (r >= 3) & (r < wide_end) & (d == 4 * (r - 2) + 3)

    def receives(d, r):
        early = (r < 3) & (lax.rem(d, 4) == r + 1)
        middle = (r >= 3) & (r < wide_end) & ((d == 4 * (r - 2)) | (d == 4 * (r - 2) + 3))
        late = (r >= wide_end) & (lax.rem(d, 4) == r - wide_end + 1) & (d >= 4)
        return early | middle | late

    def hop(r, distance):
        return pltpu.make_async_remote_copy(
            src_ref=cur, dst_ref=slots.at[r], send_sem=send.at[distance // 4],
            recv_sem=arrive.at[r], **to(lax.rem(here + distance, sections), depth),
        )

    def step(r, carry):
        one = (here + 1 < sections) & receives(here + 1, r) & jnp.logical_not(wide(here + 1, r))
        four = (here + 4 < sections) & wide(here + 4, r)

        @pl.when(one)
        def _():
            hop(r, 1).start()

        @pl.when(four)
        def _():
            hop(r, 4).start()

        @pl.when(one)
        def _():
            hop(r, 1).wait_send()

        @pl.when(four)
        def _():
            hop(r, 4).wait_send()

        @pl.when(receives(here, r))
        def _():
            hop(r, 1).wait_recv()
            before = slots[r]
            mean_square = jnp.mean(before * before, axis=-1, keepdims=True)
            normed[...] = (before * lax.rsqrt(mean_square + epsilon) * gain[...]).astype(
                jnp.bfloat16
            )
            total[...] = jnp.zeros_like(total)

            def part(i, c):
                cols = pl.ds(pl.multiple_of(i * width, width), width)
                hidden = jax.nn.gelu(
                    jnp.dot(normed[...], w_in[0, :, cols], preferred_element_type=jnp.float32),
                    approximate=True,
                ).astype(jnp.bfloat16)
                total[...] += jnp.dot(
                    hidden, w_out[0, cols, :], preferred_element_type=jnp.float32
                )
                return c

            lax.fori_loop(0, 4, part, 0)
            is_wide = wide(here, r)

            @pl.when(is_wide)
            def _():
                cur[...] = slots[r] + 16.0 * total[...] + (cur[...] - far_step[...])

            @pl.when(jnp.logical_not(is_wide))
            def _():
                cur[...] = slots[r] + 4.0 * total[...] + rhs_one[...]

        return carry

    lax.fori_loop(0, rounds, step, 0)

    def last(distance):
        return pltpu.make_async_remote_copy(
            src_ref=cur, dst_ref=ends.at[distance // 4], send_sem=send.at[distance // 4],
            recv_sem=end_arrive.at[distance // 4],
            **to(lax.rem(here + distance, sections), depth),
        )

    for distance in (1, 4):

        @pl.when(here + distance < sections)
        def _(distance=distance):
            last(distance).start()

    for k in range(1, copies):
        across_copy(k).wait()
    gathered = across[0]
    for k in range(1, copies):
        gathered = gathered + across[k]
    summed[...] = gathered

    def along_copy(k):
        return pltpu.make_async_remote_copy(
            src_ref=summed, dst_ref=along.at[k - 1],
            send_sem=along_send.at[k - 1], recv_sem=along_arrive.at[k - 1],
            **to(lax.rem(here + k, sections), depth),
        )

    for k in range(1, sections):
        along_copy(k).start()
    point[...] = cur[...]
    for distance, out, edge in ((1, left, 1), (4, far, 4)):

        @pl.when(here + distance < sections)
        def _(distance=distance):
            last(distance).wait_send()

        @pl.when(here >= edge)
        def _(distance=distance, out=out):
            last(distance).wait_recv()
            out[...] = ends[distance // 4]

        @pl.when(here < edge)
        def _(out=out):
            out[...] = initial[...]

    result = summed[...]
    for k in range(1, sections):
        along_copy(k).wait()
        result = result + along[k - 1]
    totals[...] = result


def coarse(initial, start, rhs_one, far_step, tile, gain, first_weights, second_weights):
    sections = lax.axis_size("layer")
    copies = lax.axis_size("dp")
    rounds = sections // 4 + 4
    shape = initial.shape
    d, ff = first_weights.shape[1:]
    whole = pl.BlockSpec(shape, lambda i: (0, 0))
    small = pl.BlockSpec((8, 128), lambda i: (0, 0))
    state = jax.ShapeDtypeStruct(shape, jnp.float32)
    dma = pltpu.SemaphoreType.DMA
    return pl.pallas_call(
        lambda *refs: coarse_kernel(sections, copies, *refs),
        grid=(1,),
        out_shape=(state, state, state, jax.ShapeDtypeStruct((8, 128), jnp.float32)),
        in_specs=[
            whole, whole, whole, whole, small,
            pl.BlockSpec((1, d), lambda i: (0, 0)),
            pl.BlockSpec((1, d, ff), lambda i: (3, 0, 0)),
            pl.BlockSpec((1, ff, d), lambda i: (3, 0, 0)),
        ],
        out_specs=(whole, whole, whole, small),
        scratch_shapes=[
            pltpu.VMEM(shape, jnp.float32),
            pltpu.VMEM((rounds,) + shape, jnp.float32),
            pltpu.VMEM((2,) + shape, jnp.float32),
            pltpu.VMEM(shape, jnp.bfloat16),
            pltpu.VMEM(shape, jnp.float32),
            pltpu.VMEM((copies, 8, 128), jnp.float32),
            pltpu.VMEM((sections - 1, 8, 128), jnp.float32),
            pltpu.VMEM((8, 128), jnp.float32),
            dma((2,)), dma((rounds,)), dma((2,)),
            dma((copies - 1,)), dma((copies - 1,)),
            dma((sections - 1,)), dma((sections - 1,)),
        ],
        compiler_params=pltpu.CompilerParams(
            collective_id=0, has_side_effects=True, vmem_limit_bytes=40 * 1024 * 1024
        ),
        name="coarse",
    )(initial, start, rhs_one, far_step, tile, gain, first_weights, second_weights)


def local_quads(initial, norm_gains, first_weights, second_weights):
    sections = lax.axis_size("layer")
    here = lax.axis_index("layer")
    place = here % 4
    rows = initial.shape[0]

    def moved(slot, *states):
        stacked = states[0] if len(states) == 1 else jnp.concatenate(states, axis=0)
        return branch(stacked, first_weights[slot], second_weights[slot], norm_gains[slot])

    def near(values):
        return jnp.where(here == 0, initial, shifted(values, "layer", 1))

    def distant(values):
        return jnp.where(here == 3, initial, shifted(values, "layer", 4))

    state = initial
    for slot in range(4):
        state = state + moved(slot, state)
    point = state
    left = near(point)
    far = distant(point)
    state = left
    for slot in range(3):
        state = state + moved(slot, state)
    update = moved(3, state, left, far)
    near_term = update[:rows]
    fine = state + near_term
    rhs_one = fine - (left + 4.0 * update[rows : 2 * rows])
    far_step = far + 16.0 * update[2 * rows :]
    gap = fine - point
    gap_sum = jnp.sum(gap * gap)
    step_sum = jnp.sum(near_term * near_term)

    point = jnp.where(place == 0, fine, point)
    lane = jnp.arange(128)[None, :] == here - 1
    row = jnp.arange(8)[:, None]
    tile = jnp.where(lane & (row == 0), gap_sum, 0.0) + jnp.where(lane & (row == 1), step_sum, 0.0)
    point, left, far, totals = coarse(
        initial, point, rhs_one, far_step, tile, norm_gains[3:4], first_weights, second_weights
    )
    state = left
    states = []
    for slot in range(3):
        state = state + moved(slot, state)
        states.append(state)
    states.append(point)
    inner = jnp.stack(states[:3])
    lefts = list(shifted(inner, "layer", 1)) + [left]
    fars = list(shifted(inner, "layer", 4)) + [far]
    fours = []
    sixteens = []
    for slot in range(4):
        update = moved(slot, lefts[slot], fars[slot])
        fours.append(states[slot] - (lefts[slot] + 4.0 * update[:rows]))
        sixteens.append(states[slot] - (fars[slot] + 16.0 * update[rows:]))
    points = here * 4 + jnp.arange(4, dtype=jnp.int32) + 1
    defects_four = jnp.where((points >= 4)[:, None, None], jnp.stack(fours), 0.0)
    defects_sixteen = jnp.where((points >= 16)[:, None, None], jnp.stack(sixteens), 0.0)
    gap_total = totals[0, : sections - 1]
    step_total = totals[1, : sections - 1]
    ratios = jnp.sqrt(gap_total / (step_total + epsilon))
    return (jnp.stack(states), ratios, defects_four, defects_sixteen)


def chosen(initial, norm_gains, first_weights, second_weights):
    quads = first_weights.shape[0] == 4 and lax.axis_size("layer") % 4 == 0 and lax.axis_size("dp") > 1
    return (local_quads if quads else local)(initial, norm_gains, first_weights, second_weights)


def solution(mesh):
    placed = (P("dp", None), P("layer", None), P("layer", None, None), P("layer", None, None))
    return jax.shard_map(
        chosen,
        mesh=mesh,
        in_specs=placed,
        out_specs=(P("layer", "dp", None), P(), P("layer", "dp", None), P("layer", "dp", None)),
        check_vma=False,
    )
```

profile of v0, /device:TPU:0, one launch (start us, length us, event | category | flops | bytes accessed | tf_op | source)
XLA Modules:
  0.0 184.4 jit_solution(10556816134786441955)
XLA Ops:
  0.6 0.9 fusion.543
  1.5 1.1 multiply_reduce_fusion.16
  2.6 5.4 %multiply_reduce_fusion.15 = (f32[64]{0:T(128)S(1)}, f32[64,1024]{1,0:T(8,128)S(1)}) fusion(f32[64,1024]{1,0:T(8,128)} %refs_0_.1, bf16[4,2048,1024]{2,1,0:T(8,128)(2,1)} %refs_7_.1, bf16[4,1024,2048]{2,1,0:T(8,128)(2,1)} %refs_6_.1, f32[1024]{0:T(1024)S(1)} %bitcast.266, f32[64]{0:T(128)S(1)} %add_rsqrt_fusion.14), kind=kOutput, calls=%fused_computation.341 | convolution fusion | flops 538443712 | bytes 9179648 | tf_op jit(solution)/shard_map/dot_general | solution.py:23
  8.0 0.0 copy-start
  8.0 5.4 %multiply_reduce_fusion.14 = (f32[64]{0:T(128)S(1)}, f32[64,1024]{1,0:T(8,128)S(1)}) fusion(f32[64,1024]{1,0:T(8,128)S(1)} %get-tuple-element.40, bf16[4,2048,1024]{2,1,0:T(8,128)(2,1)} %refs_7_.1, bf16[4,1024,2048]{2,1,0:T(8,128)(2,1)} %refs_6_.1, f32[1024]{0:T(1024)S(1)} %bitcast.274, f32[64]{0:T(128)S(1)} %add_rsqrt_fusion.13), kind=kOutput, calls=%fused_computation.339 | convolution fusion | flops 538443712 | bytes 9179904 | tf_op jit(solution)/shard_map/dot_general | solution.py:23
  13.4 5.3 %multiply_reduce_fusion.13 = (f32[64]{0:T(128)S(1)}, f32[64,1024]{1,0:T(8,128)S(1)}) fusion(f32[64,1024]{1,0:T(8,128)S(1)} %get-tuple-element.42, bf16[4,2048,1024]{2,1,0:T(8,128)(2,1)} %refs_7_.1, bf16[4,1024,2048]{2,1,0:T(8,128)(2,1)} %refs_6_.1, f32[1024]{0:T(1024)S(1)} %bitcast.270, f32[64]{0:T(128)S(1)} %add_rsqrt_fusion.12), kind=kOutput, calls=%fused_computation.337 | convolution fusion | flops 538443712 | bytes 9179904 | tf_op jit(solution)/shard_map/dot_general | solution.py:23
  18.8 5.2 %fusion.129 = f32[64,1024]{1,0:T(8,128)S(1)} fusion(f32[64,1024]{1,0:T(8,128)S(1)} %get-tuple-element.44, bf16[4,2048,1024]{2,1,0:T(8,128)(2,1)} %refs_7_.1, bf16[4,1024,2048]{2,1,0:T(8,128)(2,1)} %refs_6_.1, f32[1024]{0:T(1024)S(1)} %bitcast.257, f32[64]{0:T(128)S(1)} %add_rsqrt_fusion.11), kind=kOutput, calls=%fused_computation.112 | convolution fusion | flops 538312704 | bytes 9179648 | tf_op jit(solution)/shard_map/dot_general | solution.py:23
  24.0 2.4 %collective-permute-start = (f32[64,1024]{1,0:T(8,128)S(1)}, f32[64,1024]{1,0:T(8,128)S(1)}, u32[]{:S(2)}, u32[]{:S(2)}) collective-permute-start(f32[64,1024]{1,0:T(8,128)S(1)} %fusion.129), channel_id=1, source_target_pairs={{0,4},{4,8},{8,12},{12,16},{16,20},{20,24},{24,28},{1,5},{5,9},{9,... | collective-permute-start | bytes 786440 | tf_op jit(solution)/shard_map/ppermute | solution.py:14
  26.4 4.6 %collective-permute-start.1 = (f32[64,1024]{1,0:T(8,128)S(1)}, f32[64,1024]{1,0:T(8,128)S(1)}, u32[]{:S(2)}, u32[]{:S(2)}) collective-permute-start(f32[64,1024]{1,0:T(8,128)S(1)} %fusion.129), channel_id=1, source_target_pairs={{0,16},{4,20},{8,24},{12,28},{1,17},{5,21},{9,25},{13,29},{2,18},{... | collective-permute-start | bytes 786440 | tf_op jit(solution)/shard_map/ppermute | solution.py:14
  31.1 0.0 collective-permute-done
  31.1 7.6 %collective-permute-done.1 = f32[64,1024]{1,0:T(8,128)S(1)} collective-permute-done((f32[64,1024]{1,0:T(8,128)S(1)}, f32[64,1024]{1,0:T(8,128)S(1)}, u32[]{:S(2)}, u32[]{:S(2)}) %collective-permute-start.1) | collective-permute-done | bytes 262176 | tf_op jit(solution)/shard_map/ppermute | solution.py:14
  38.7 0.0 copy-done
  38.7 0.1 multiply_reduce_fusion.12
  38.8 5.3 %multiply_reduce_fusion.11 = (f32[64]{0:T(128)S(1)}, f32[64,1024]{1,0:T(8,128)S(1)}) fusion(f32[64,1024]{1,0:T(8,128)S(1)} %get-tuple-element.15, bf16[4,2048,1024]{2,1,0:T(8,128)(2,1)} %refs_7_.1, bf16[4,1024,2048]{2,1,0:T(8,128)(2,1)} %refs_6_.1, f32[64]{0:T(128)S(1)} %add_rsqrt_fusion.10, f32[1024]{0:T(1024)S(1)} %bitcast.267), kind=kOutput, calls=%fused_computation.333 | convolution fusion | flops 538443712 | bytes 9179904 | tf_op jit(solution)/shard_map/dot_general | solution.py:23
  44.2 5.3 %multiply_reduce_fusion.10 = (f32[64]{0:T(128)S(1)}, f32[64,1024]{1,0:T(8,128)S(1)}) fusion(f32[64,1024]{1,0:T(8,128)S(1)} %get-tuple-element.46, bf16[4,2048,1024]{2,1,0:T(8,128)(2,1)} %refs_7_.1, bf16[4,1024,2048]{2,1,0:T(8,128)(2,1)} %refs_6_.1, f32[64]{0:T(128)S(1)} %add_rsqrt_fusion.9, f32[1024]{0:T(1024)S(1)} %bitcast.275), kind=kOutput, calls=%fused_computation.331 | convolution fusion | flops 538443712 | bytes 9179904 | tf_op jit(solution)/shard_map/dot_general | solution.py:23
  49.5 5.2 %fusion.123 = f32[64,1024]{1,0:T(8,128)S(1)} fusion(f32[64,1024]{1,0:T(8,128)S(1)} %get-tuple-element.48, bf16[4,2048,1024]{2,1,0:T(8,128)(2,1)} %refs_7_.1, bf16[4,1024,2048]{2,1,0:T(8,128)(2,1)} %refs_6_.1, f32[64]{0:T(128)S(1)} %add_rsqrt_fusion.8, f32[1024]{0:T(1024)S(1)} %bitcast.271), kind=kOutput, calls=%fused_computation.110 | convolution fusion | flops 538312704 | bytes 9179648 | tf_op jit(solution)/shard_map/dot_general | solution.py:23
  54.8 0.1 multiply_reduce_fusion
  54.9 5.7 %fusion.2 = f32[192,1024]{1,0:T(8,128)S(1)} fusion(bf16[4,2048,1024]{2,1,0:T(8,128)(2,1)} %refs_7_.1, bf16[4,1024,2048]{2,1,0:T(8,128)(2,1)} %refs_6_.1, f32[64,1024]{1,0:T(8,128)S(1)} %get-tuple-element.34, f32[64,1024]{1,0:T(8,128)S(1)} %get-tuple-element.15, f32[64,1024]{1,0:T(8,128)S(1)} %fusion.123, f32[1024]{0:T(1024)S(1)} %bitcast.258, ...), kind=kOutput, calls=%fused_computation.2 | convolution fusion | flops 1615134720 | bytes 9966336 | tf_op jit(solution)/shard_map/dot_general | solution.py:23
  60.6 0.7 multiply_reduce_fusion.9
  61.4 1.4 select_add_fusion.refs_4_
  62.7 45.2 %coarse.1 = (f32[64,1024]{1,0:T(8,128)S(1)}, f32[64,1024]{1,0:T(8,128)S(1)}, f32[64,1024]{1,0:T(8,128)S(1)}, f32[8,128]{1,0:T(8,128)S(1)}) custom-call(f32[64,1024]{1,0:T(8,128)S(1)} %copy-done, f32[64,1024]{1,0:T(8,128)S(1)} %get-tuple-element.16.refs_1_, f32[64,1024]{1,0:T(8,128)S(1)} %get-tuple-element.17.refs_2_, ...), custom_call_target="tpu_custom_call" | custom-call | tf_op jit(solution)/shard_map/coarse/pallas_call | solution.py:361
  108.0 0.1 multiply_reduce_fusion.1
  108.1 5.1 %fusion = f32[128,1024]{1,0:T(8,128)S(1)} fusion(bf16[4,2048,1024]{2,1,0:T(8,128)(2,1)} %refs_7_.1, bf16[4,1024,2048]{2,1,0:T(8,128)(2,1)} %refs_6_.1, f32[128,1024]{1,0:T(8,128)S(1)} %constant_dynamic-update-slice_fusion, f32[1024]{0:T(1024)S(1)} %bitcast.259, f32[128]{0:T(128)S(1)} %add_rsqrt_fusion.1), kind=kOutput, calls=%fused_computation | convolution fusion | flops 1076494336 | bytes 9441792 | tf_op jit(solution)/shard_map/dot_general | solution.py:23
  113.2 0.2 fusion.352
  113.4 5.3 %multiply_reduce_fusion.6 = (f32[64]{0:T(128)S(1)}, f32[64,1024]{1,0:T(8,128)S(1)}) fusion(f32[64,1024]{1,0:T(8,128)S(1)} %get-tuple-element.8, bf16[4,2048,1024]{2,1,0:T(8,128)(2,1)} %refs_7_.1, bf16[4,1024,2048]{2,1,0:T(8,128)(2,1)} %refs_6_.1, f32[64]{0:T(128)S(1)} %add_rsqrt_fusion.7, f32[1024]{0:T(1024)S(1)} %bitcast.268), kind=kOutput, calls=%fused_computation.325 | convolution fusion | flops 538443712 | bytes 9179904 | tf_op jit(solution)/shard_map/dot_general | solution.py:23
  118.7 5.3 %multiply_reduce_fusion.5 = (f32[64]{0:T(128)S(1)}, f32[64,1024]{1,0:T(8,128)S(1)}) fusion(f32[64,1024]{1,0:T(8,128)S(1)} %get-tuple-element.50, bf16[4,2048,1024]{2,1,0:T(8,128)(2,1)} %refs_7_.1, bf16[4,1024,2048]{2,1,0:T(8,128)(2,1)} %refs_6_.1, f32[64]{0:T(128)S(1)} %add_rsqrt_fusion.6, f32[1024]{0:T(1024)S(1)} %bitcast.276), kind=kOutput, calls=%fused_computation.323 | convolution fusion | flops 538443712 | bytes 9179904 | tf_op jit(solution)/shard_map/dot_general | solution.py:23
  124.1 5.2 %fusion.126 = f32[64,1024]{1,0:T(8,128)S(1)} fusion(f32[64,1024]{1,0:T(8,128)S(1)} %get-tuple-element.52, bf16[4,2048,1024]{2,1,0:T(8,128)(2,1)} %refs_7_.1, bf16[4,1024,2048]{2,1,0:T(8,128)(2,1)} %refs_6_.1, f32[64]{0:T(128)S(1)} %add_rsqrt_fusion.5, f32[1024]{0:T(1024)S(1)} %bitcast.272), kind=kOutput, calls=%fused_computation.111 | convolution fusion | flops 538312704 | bytes 9179648 | tf_op jit(solution)/shard_map/dot_general | solution.py:23
  129.3 0.9 pad_maximum_fusion.2
  130.2 2.1 %collective-permute-start.2 = (f32[3,64,1024]{2,1,0:T(8,128)}, f32[3,64,1024]{2,1,0:T(8,128)S(1)}, u32[]{:S(2)}, u32[]{:S(2)}) collective-permute-start(f32[3,64,1024]{2,1,0:T(8,128)} %pad_maximum_fusion.2), channel_id=1, source_target_pairs={{0,4},{4,8},{8,12},{12,16},{16,20},{20,24},{24,28},{1,5},{5,9},{9,... | collective-permute-start | bytes 2359304 | tf_op jit(solution)/shard_map/ppermute | solution.py:14
  132.3 2.5 %collective-permute-start.3 = (f32[3,64,1024]{2,1,0:T(8,128)}, f32[3,64,1024]{2,1,0:T(8,128)S(1)}, u32[]{:S(2)}, u32[]{:S(2)}) collective-permute-start(f32[3,64,1024]{2,1,0:T(8,128)} %pad_maximum_fusion.2), channel_id=1, source_target_pairs={{0,16},{4,20},{8,24},{12,28},{1,17},{5,21},{9,25},{13,29},{2,18},{... | collective-permute-start | bytes 2359304 | tf_op jit(solution)/shard_map/ppermute | solution.py:14
  134.9 1.1 pad_maximum_fusion
  135.9 0.5 sqrt_bitcast_fusion
  136.4 0.0 collective-permute-done.2
  136.4 0.8 slice_bitcast_fusion.5
  137.2 0.0 copy-start.1
  137.2 22.5 %collective-permute-done.3 = f32[3,64,1024]{2,1,0:T(8,128)S(1)} collective-permute-done((f32[3,64,1024]{2,1,0:T(8,128)}, f32[3,64,1024]{2,1,0:T(8,128)S(1)}, u32[]{:S(2)}, u32[]{:S(2)}) %collective-permute-start.3) | collective-permute-done | bytes 786464 | tf_op jit(solution)/shard_map/ppermute | solution.py:14
  159.8 0.8 slice_bitcast_fusion.4
  160.5 0.0 copy-start.2
  160.5 0.0 copy-done.1
  160.5 0.1 multiply_reduce_fusion.3
  160.6 0.6 copy-done.2
  161.2 6.0 %fusion.28 = f32[128,1024]{1,0:T(8,128)} fusion(bf16[4,2048,1024]{2,1,0:T(8,128)(2,1)} %refs_7_.1, bf16[4,1024,2048]{2,1,0:T(8,128)(2,1)} %refs_6_.1, f32[64,1024]{1,0:T(8,128)} %copy-done.2, f32[64,1024]{1,0:T(8,128)} %copy-done.1, f32[1024]{0:T(1024)S(1)} %bitcast.277, f32[128]{0:T(128)S(1)} %add_rsqrt_fusion.3), kind=kOutput, calls=%fused_computation.28 | convolution fusion | flops 1076625408 | bytes 9441792 | tf_op jit(solution)/shard_map/dot_general | solution.py:23
  167.3 1.1 multiply_reduce_fusion.2
  168.4 6.0 %fusion.12 = f32[128,1024]{1,0:T(8,128)} fusion(bf16[4,2048,1024]{2,1,0:T(8,128)(2,1)} %refs_7_.1, bf16[4,1024,2048]{2,1,0:T(8,128)(2,1)} %refs_6_.1, f32[64,1024]{1,0:T(8,128)} %get-tuple-element.30, f32[64,1024]{1,0:T(8,128)} %get-tuple-element.27, f32[1024]{0:T(1024)S(1)} %bitcast.273, f32[128]{0:T(128)S(1)} %add_rsqrt_fusion.2), kind=kOutput, calls=%fused_computation.12 | convolution fusion | flops 1076625408 | bytes 9441792 | tf_op jit(solution)/shard_map/dot_general | solution.py:23
  174.4 0.1 multiply_reduce_fusion.4
  174.6 5.9 %fusion.44 = f32[128,1024]{1,0:T(8,128)} fusion(bf16[4,2048,1024]{2,1,0:T(8,128)(2,1)} %refs_7_.1, bf16[4,1024,2048]{2,1,0:T(8,128)(2,1)} %refs_6_.1, f32[64,1024]{1,0:T(8,128)S(1)} %get-tuple-element.29, f32[64,1024]{1,0:T(8,128)S(1)} %get-tuple-element.26, f32[1024]{0:T(1024)S(1)} %bitcast.269, f32[128]{0:T(128)S(1)} %add_rsqrt_fusion.4), kind=kOutput, calls=%fused_computation.44 | convolution fusion | flops 1076625408 | bytes 9441792 | tf_op jit(solution)/shard_map/dot_general | solution.py:23
  180.4 1.7 fusion.361
  182.1 1.2 maximum_select_fusion.1
  183.3 1.2 maximum_select_fusion
  (20 shorter events, 0.2 us)
Async XLA Ops:
  8.0 30.6 %copy-start = (f32[64,1024]{1,0:T(8,128)S(1)}, f32[64,1024]{1,0:T(8,128)}, u32[]{:S(2)}) copy-start(f32[64,1024]{1,0:T(8,128)} %refs_0_.1) | copy-start | bytes 786436
  24.0 7.1 %collective-permute-start = (f32[64,1024]{1,0:T(8,128)S(1)}, f32[64,1024]{1,0:T(8,128)S(1)}, u32[]{:S(2)}, u32[]{:S(2)}) collective-permute-start(f32[64,1024]{1,0:T(8,128)S(1)} %fusion.129), channel_id=1, source_target_pairs={{0,4},{4,8},{8,12},{12,16},{16,20},{20,24},{24,28},{1,5},{5,9},{9,... | collective-permute-start | bytes 786440 | tf_op jit(solution)/shard_map/ppermute | solution.py:14
  26.4 12.2 %collective-permute-start.1 = (f32[64,1024]{1,0:T(8,128)S(1)}, f32[64,1024]{1,0:T(8,128)S(1)}, u32[]{:S(2)}, u32[]{:S(2)}) collective-permute-start(f32[64,1024]{1,0:T(8,128)S(1)} %fusion.129), channel_id=1, source_target_pairs={{0,16},{4,20},{8,24},{12,28},{1,17},{5,21},{9,25},{13,29},{2,18},{... | collective-permute-start | bytes 786440 | tf_op jit(solution)/shard_map/ppermute | solution.py:14
  130.2 6.2 %collective-permute-start.2 = (f32[3,64,1024]{2,1,0:T(8,128)}, f32[3,64,1024]{2,1,0:T(8,128)S(1)}, u32[]{:S(2)}, u32[]{:S(2)}) collective-permute-start(f32[3,64,1024]{2,1,0:T(8,128)} %pad_maximum_fusion.2), channel_id=1, source_target_pairs={{0,4},{4,8},{8,12},{12,16},{16,20},{20,24},{24,28},{1,5},{5,9},{9,... | collective-permute-start | bytes 2359304 | tf_op jit(solution)/shard_map/ppermute | solution.py:14
  132.3 27.5 %collective-permute-start.3 = (f32[3,64,1024]{2,1,0:T(8,128)}, f32[3,64,1024]{2,1,0:T(8,128)S(1)}, u32[]{:S(2)}, u32[]{:S(2)}) collective-permute-start(f32[3,64,1024]{2,1,0:T(8,128)} %pad_maximum_fusion.2), channel_id=1, source_target_pairs={{0,16},{4,20},{8,24},{12,28},{1,17},{5,21},{9,25},{13,29},{2,18},{... | collective-permute-start | bytes 2359304 | tf_op jit(solution)/shard_map/ppermute | solution.py:14
  137.2 23.3 %copy-start.1 = (f32[64,1024]{1,0:T(8,128)}, f32[64,1024]{1,0:T(8,128)S(1)}, u32[]{:S(2)}) copy-start(f32[64,1024]{1,0:T(8,128)S(1)} %get-tuple-element.28) | copy-start | bytes 786436
  160.5 0.7 copy-start.2
where the time goes:
time: 185 us; the launch traced here: 184 us
  matrix products  81.8 us (44%)
  Pallas kernels  45.2 us (24%)
  waiting for transfers between devices  30.1 us (16%)
  other arithmetic  11.8 us (6%)
  starting transfers between devices  11.6 us (6%)
  local copies, waits for them, and re-layouts  3.06 us (2%)
    dot_general x15, matrix products, branch(): return jnp.dot(hidden, weight_out, preferred_element_type=jnp.float32)  81.8 us
    pallas_call x1, Pallas kernels, coarse(): pl.pallas_call(lambda *refs: coarse_kernel(sections, copies, *refs), grid...  45.2 us
    ppermute x4, waiting for transfers between devices, shifted(): return lax.ppermute(block, axis, route)  30.1 us
    ppermute x4, starting transfers between devices, shifted(): return lax.ppermute(block, axis, route)  11.6 us
  transfers between devices with their start and end apart: 4, of which 2 were waited for; matrix products, arithmetic and copies ran while one was open for 1% of the time, Pallas kernels for 0%

commit v1 on v0

v1 whole, which is shorter than its diff:
```python
import jax
import jax.numpy as jnp
from jax import lax
from jax.experimental import pallas as pl
from jax.experimental.pallas import tpu as pltpu
from jax.sharding import PartitionSpec as P

epsilon = 1e-06


def shifted(block, axis, distance):
    devices = range(lax.axis_size(axis))
    route = [(i - distance, i) for i in devices if i - distance in devices]
    return lax.ppermute(block, axis, route)


def branch(row_block, weight_in, weight_out, gain_row):
    mean_square = jnp.mean(row_block * row_block, axis=-1, keepdims=True)
    normed = (row_block * lax.rsqrt(mean_square + epsilon) * gain_row).astype(jnp.bfloat16)
    hidden = jax.nn.gelu(
        jnp.dot(normed, weight_in, preferred_element_type=jnp.float32), approximate=True
    ).astype(jnp.bfloat16)
    return jnp.dot(hidden, weight_out, preferred_element_type=jnp.float32)


def local(initial, norm_gains, first_weights, second_weights):
    slot_count = first_weights.shape[0]
    sections = lax.axis_size("layer")
    layer_total = slot_count * sections
    norm_count = layer_total // 4 - 1
    first_point = lax.axis_index("layer") * slot_count
    points = first_point + jnp.arange(slot_count, dtype=jnp.int32) + 1
    spacings = (1, 4, 16)

    def shaped(flags, rank):
        return flags.reshape((slot_count,) + (1,) * (rank - 1))

    def previous(values, level_index):
        spacing = spacings[level_index]
        if spacing >= slot_count:
            portion = values
            distance = spacing // slot_count
        else:
            portion = values[slot_count - spacing :]
            distance = 1
        if level_index == 0:
            arrived = shifted(portion, "layer", distance)
        elif level_index == 1:
            arrived = shifted(portion, "layer", distance)
        else:
            arrived = shifted(portion, "layer", distance)
        if spacing < slot_count:
            arrived = jnp.concatenate([arrived, values[: slot_count - spacing]], axis=0)
        return arrived

    def incoming(values, level_index, anchor):
        arrived = previous(values, level_index)
        from_anchor = shaped(points - spacings[level_index] == 0, values.ndim)
        return jnp.where(from_anchor, anchor, arrived)

    def advance(before, level_index, active, right_side):
        factor = float(spacings[level_index])
        results = []
        for slot in range(slot_count):

            def advance_compute(values, source, slot=slot):
                return (
                    values
                    + factor
                    * branch(values, first_weights[slot], second_weights[slot], norm_gains[slot])
                    + source
                )

            def advance_unchanged(values, source):
                return values

            source = right_side[slot] if right_side is not None else jnp.zeros_like(before[slot])
            results.append(
                lax.cond(active[slot], advance_compute, advance_unchanged, before[slot], source)
            )
        return jnp.stack(results)

    def relaxation(current, level_index, residues, right_side, anchor):
        modulus = 4 * spacings[level_index]
        for residue in residues:
            before = incoming(current, level_index, anchor)
            active = points % modulus == residue
            current = jnp.where(
                shaped(active, 3), advance(before, level_index, active, right_side), current
            )
        return (current, None)

    def restrict(current, level_index, right_side, anchor):
        spacing = spacings[level_index]
        factor = float(spacing)
        wide_factor = float(4 * spacing)
        before = incoming(current, level_index, anchor)
        far_state = incoming(current, level_index + 1, anchor)
        active = points % (4 * spacing) == 0
        row_count = current.shape[1]
        coarse_list = []
        gap_list = []
        step_list = []
        for slot in range(slot_count):

            def restrict_compute(near, distant, held, source, slot=slot):
                update = branch(
                    jnp.concatenate([near, distant], axis=0),
                    first_weights[slot],
                    second_weights[slot],
                    norm_gains[slot],
                )
                near_term = update[:row_count]
                fine_value = near + factor * near_term + source
                coarse = fine_value - (distant + wide_factor * update[row_count:])
                gap = fine_value - held
                return (coarse, jnp.sum(gap * gap), jnp.sum(near_term * near_term))

            def restrict_unchanged(near, distant, held, source):
                nothing = jnp.zeros((), near.dtype)
                return (jnp.zeros_like(near), nothing, nothing)

            source = right_side[slot] if right_side is not None else jnp.zeros_like(before[slot])
            coarse, gap_sum, step_sum = lax.cond(
                active[slot],
                restrict_compute,
                restrict_unchanged,
                before[slot],
                far_state[slot],
                current[slot],
                source,
            )
            coarse_list.append(coarse)
            gap_list.append(gap_sum)
            step_list.append(step_sum)
        return (jnp.stack(coarse_list), jnp.stack(gap_list), jnp.stack(step_list))

    def defects(current, level_index, anchor):
        spacing = spacings[level_index]
        factor = float(spacing)
        before = incoming(current, level_index, anchor)
        stepped = []
        for slot in range(slot_count):
            stepped.append(
                before[slot]
                + factor
                * branch(before[slot], first_weights[slot], second_weights[slot], norm_gains[slot])
            )
        valid = shaped(points >= spacing, 3)
        return jnp.where(valid, current - jnp.stack(stepped), 0.0)

    def multigrid_cycle(anchor):
        current = jnp.broadcast_to(anchor, (slot_count,) + anchor.shape)
        current, unused = relaxation(current, 0, (1, 2, 3), None, anchor)
        current, unused = relaxation(current, 0, (0,), None, anchor)
        current, carried = relaxation(current, 0, (1, 2, 3), None, anchor)
        rhs_one, gap_sums, step_sums = restrict(current, 0, None, anchor)
        current, carried = relaxation(current, 1, (4, 8, 12), rhs_one, anchor)
        rhs_two, unused_gaps, unused_steps = restrict(current, 1, rhs_one, anchor)
        for coarse_step in range(1, layer_total // 16 + 1):
            active = points == 16 * coarse_step
            before = incoming(current, 2, anchor)
            current = jnp.where(shaped(active, 3), advance(before, 2, active, rhs_two), current)
        current, unused = relaxation(current, 1, (4, 8, 12), rhs_one, anchor)
        current, unused = relaxation(current, 0, (1, 2, 3), None, anchor)
        defects_four = defects(current, 1, anchor)
        defects_sixteen = defects(current, 2, anchor)
        return (current, gap_sums, step_sums, defects_four, defects_sixteen)

    portions = [initial]
    outcomes = [multigrid_cycle(portion) for portion in portions]
    layer_states = jnp.concatenate([outcome[0] for outcome in outcomes], axis=1)
    defects_four = jnp.concatenate([outcome[3] for outcome in outcomes], axis=1)
    defects_sixteen = jnp.concatenate([outcome[4] for outcome in outcomes], axis=1)
    gap_sums = outcomes[0][1]
    step_sums = outcomes[0][2]
    counted = (points % 4 == 0) & (points >= 8)
    entry_index = points // 4 - 2
    one_hot = (
        (jnp.arange(norm_count, dtype=jnp.int32)[None, :] == entry_index[:, None])
        & counted[:, None]
    ).astype(jnp.float32)
    gap_vector = jnp.sum(gap_sums[:, None] * one_hot, axis=0)
    step_vector = jnp.sum(step_sums[:, None] * one_hot, axis=0)
    gap_total, step_total = lax.psum((gap_vector, step_vector), ("layer", "dp"))
    residual_ratios = jnp.sqrt(gap_total / (step_total + epsilon))
    return (layer_states, residual_ratios, defects_four, defects_sixteen)


def cycle_kernel(
    sections, copies,
    initial, norm_gains, first_weights, second_weights,
    out_states, out_four, out_sixteen, ratios,
    w_in, w_out, gain, start, normed, hidden, total, cur,
    relaxed, middle, final, rhs, wide_start,
    left_relaxed, left_middle, left_final, far_relaxed, far_final, lefts, fars,
    states, four, sixteen, tile, across, along, summed,
    load_in, load_out, load_small, store,
    send_point, take_point, send_state, take_state,
    across_send, across_take, along_send, along_take,
):
    here = lax.axis_index("layer")
    depth = lax.axis_index("dp")
    slot_count, width, ff = w_in.shape
    rows = start.shape[0]
    half = sections // 2
    end = sections - 1
    slot_last = slot_count - 1

    def to(layer, dp):
        return dict(device_id=(layer, dp), device_id_type=pl.DeviceIdType.MESH)

    def load_first(slot):
        return pltpu.make_async_copy(first_weights.at[slot], w_in.at[slot], load_in.at[slot])

    def load_second(slot):
        return pltpu.make_async_copy(second_weights.at[slot], w_out.at[slot], load_out.at[slot])

    load_start = pltpu.make_async_copy(initial, start, load_small.at[0])
    load_gain = pltpu.make_async_copy(norm_gains, gain, load_small.at[1])
    load_start.start()
    load_gain.start()
    for slot in range(slot_count):
        load_first(slot).start()
        load_second(slot).start()

    barrier = pltpu.get_barrier_semaphore()
    for k in range(1, sections):
        pl.semaphore_signal(barrier, inc=1, **to(lax.rem(here + k, sections), depth))
    for k in range(1, copies):
        pl.semaphore_signal(barrier, inc=1, **to(here, lax.rem(depth + k, copies)))

    def point_send(kind, source, target, distance):
        return pltpu.make_async_remote_copy(
            src_ref=source, dst_ref=target,
            send_sem=send_point.at[kind], recv_sem=take_point.at[kind],
            **to(lax.rem(here + distance, sections), depth),
        )

    give_relaxed = point_send(0, relaxed, left_relaxed, 1)
    give_far_relaxed = point_send(1, relaxed, far_relaxed, half)
    give_middle = point_send(2, middle, left_middle, 1)
    give_final = point_send(3, final, left_final, 1)
    give_far_final = point_send(4, final, far_final, half)

    def state_send(slot, target, distance, row):
        return pltpu.make_async_remote_copy(
            src_ref=states.at[slot], dst_ref=target.at[slot],
            send_sem=send_state.at[row, slot], recv_sem=take_state.at[row, slot],
            **to(lax.rem(here + distance, sections), depth),
        )

    def give_left(slot):
        return state_send(slot, lefts, 1, 0)

    def give_far(slot):
        return state_send(slot, fars, half, 1)

    def across_copy(k):
        return pltpu.make_async_remote_copy(
            src_ref=tile, dst_ref=across.at[depth],
            send_sem=across_send.at[k - 1], recv_sem=across_take.at[k - 1],
            **to(here, lax.rem(depth + k, copies)),
        )

    def along_copy(k):
        return pltpu.make_async_remote_copy(
            src_ref=summed, dst_ref=along.at[k - 1],
            send_sem=along_send.at[k - 1], recv_sem=along_take.at[k - 1],
            **to(lax.rem(here + k, sections), depth),
        )

    def normalise(part, values, slot):
        mean_square = jnp.mean(values * values, axis=-1, keepdims=True)
        normed[part * rows : (part + 1) * rows, :] = (
            values * lax.rsqrt(mean_square + epsilon) * gain[pl.ds(slot, 1), :]
        ).astype(jnp.bfloat16)

    def project_in(parts, slot):
        step = ff // 4
        for i in range(4):
            cols = slice(i * step, (i + 1) * step)
            hidden[: parts * rows, cols] = jax.nn.gelu(
                jnp.dot(
                    normed[: parts * rows, :], w_in[slot, :, cols],
                    preferred_element_type=jnp.float32,
                ),
                approximate=True,
            ).astype(jnp.bfloat16)

    def project_out(parts, slot):
        step = width // 4
        for i in range(4):
            cols = slice(i * step, (i + 1) * step)
            total[: parts * rows, cols] = jnp.dot(
                hidden[: parts * rows, :], w_out[slot, :, cols],
                preferred_element_type=jnp.float32,
            )

    def update(part):
        return total[part * rows : (part + 1) * rows, :]

    load_start.wait()
    load_gain.wait()
    cur[...] = start[...]

    def first_pass(slot, carry):
        normalise(0, cur[...], slot)
        normalise(1, start[...], slot)
        load_first(slot).wait()
        project_in(2, slot)
        load_second(slot).wait()
        project_out(2, slot)
        state = cur[...] + update(0)
        cur[...] = state
        states[slot] = state
        return carry

    lax.fori_loop(0, slot_count, first_pass, 0)
    relaxed[...] = cur[...]
    pl.semaphore_wait(barrier, sections + copies - 2)

    @pl.when(here < end)
    def _():
        give_relaxed.start()

    @pl.when(here == half - 1)
    def _():
        give_far_relaxed.start()

    four[...] = jnp.zeros_like(four)
    sixteen[...] = jnp.zeros_like(sixteen)
    tile[...] = jnp.zeros_like(tile)

    @pl.when(here == half - 1)
    def _():
        wide_start[...] = start[...] + 16.0 * update(1)

    @pl.when(here == 0)
    def _():
        final[...] = relaxed[...]
        give_far_final.start()
        four[slot_last] = relaxed[...] - (start[...] + 4.0 * update(1))
        for slot in range(slot_last):
            give_left(slot).start()
            give_far(slot).start()

    @pl.when(here > 0)
    def _():
        give_relaxed.wait_recv()
        cur[...] = left_relaxed[...]

        def second_pass(slot, carry):
            normalise(0, cur[...], slot)

            @pl.when(slot == slot_last)
            def _():
                normalise(1, left_relaxed[...], slot)

            project_in(2, slot)
            project_out(2, slot)
            state = cur[...] + update(0)
            cur[...] = state
            states[slot] = state
            return carry

        lax.fori_loop(0, slot_count, second_pass, 0)

        @pl.when(here == 1)
        def _():
            final[...] = cur[...]
            give_final.start()
            give_far_final.start()
            for slot in range(slot_last):
                give_left(slot).start()
                give_far(slot).start()

        @pl.when(here == half)
        def _():
            middle[...] = cur[...]
            give_middle.start()

        fine = cur[...]
        source = fine - (left_relaxed[...] + 4.0 * update(1))
        rhs[...] = source

        @pl.when(here == 1)
        def _():
            four[slot_last] = source

        gap = fine - relaxed[...]
        near_term = update(0)
        lane = lax.broadcasted_iota(jnp.int32, tile.shape, 1) == here - 1
        row = lax.broadcasted_iota(jnp.int32, tile.shape, 0)
        tile[...] = jnp.where(lane & (row == 0), jnp.sum(gap * gap), 0.0) + jnp.where(
            lane & (row == 1), jnp.sum(near_term * near_term), 0.0
        )

    across[depth] = tile[...]
    for k in range(1, copies):
        across_copy(k).start()

    def coarse_pass(r, carry):
        middle_round = (r == 0) & (here > half)
        wide_round = (r == 1) & (here == end)
        final_round = (r == 2) & (here > 1)

        @pl.when(middle_round | wide_round | final_round)
        def _():
            @pl.when(middle_round)
            def _():
                give_middle.wait_recv()
                normalise(0, left_middle[...], slot_last)

            @pl.when(wide_round)
            def _():
                give_far_relaxed.wait_recv()
                normalise(1, far_relaxed[...], slot_last)
                give_far_final.wait_recv()
                normalise(0, far_final[...], slot_last)

            @pl.when(final_round)
            def _():
                @pl.when((here >= half) & (here < end))
                def _():
                    give_far_final.wait_recv()
                    normalise(1, far_final[...], slot_last)

                give_final.wait_recv()
                normalise(0, left_final[...], slot_last)

            project_in(2, slot_last)
            project_out(2, slot_last)

            @pl.when(middle_round)
            def _():
                middle[...] = left_middle[...] + 4.0 * update(0) + rhs[...]

                @pl.when(here < end)
                def _():
                    give_middle.start()

            @pl.when(wide_round)
            def _():
                stepped = far_final[...] + 16.0 * update(0)
                point = stepped + (middle[...] - (far_relaxed[...] + 16.0 * update(1)))
                final[...] = point
                sixteen[slot_last] = point - stepped

            @pl.when(final_round)
            def _():
                stepped = left_final[...] + 4.0 * update(0)

                @pl.when(here < end)
                def _():
                    final[...] = stepped + rhs[...]
                    give_final.start()

                @pl.when(here < half)
                def _():
                    give_far_final.start()

                point = final[...]
                four[slot_last] = point - stepped

                @pl.when(here == half - 1)
                def _():
                    sixteen[slot_last] = point - wide_start[...]

                @pl.when((here >= half) & (here < end))
                def _():
                    sixteen[slot_last] = point - (far_final[...] + 16.0 * update(1))

        return carry

    lax.fori_loop(0, 3, coarse_pass, 0)

    for k in range(1, copies):
        across_copy(k).wait()
    gathered = across[0]
    for k in range(1, copies):
        gathered = gathered + across[k]
    summed[...] = gathered
    for k in range(1, sections):
        along_copy(k).start()

    states[slot_last] = final[...]

    @pl.when(here > 0)
    def _():
        @pl.when(here > 1)
        def _():
            cur[...] = left_final[...]

        def last_pass(slot, carry):
            @pl.when(here > 1)
            def _():
                normalise(0, cur[...], slot)

            give_left(slot).wait_recv()
            normalise(1, lefts[slot], slot)

            @pl.when(here >= half)
            def _():
                give_far(slot).wait_recv()
                normalise(2, fars[slot], slot)

            project_in(3, slot)
            project_out(3, slot)

            @pl.when(here > 1)
            def _():
                state = cur[...] + update(0)
                cur[...] = state
                states[slot] = state

                @pl.when(here < end)
                def _():
                    give_left(slot).start()

                @pl.when(here < half)
                def _():
                    give_far(slot).start()

            state = states[slot]
            four[slot] = state - (lefts[slot] + 4.0 * update(1))

            @pl.when(here >= half)
            def _():
                sixteen[slot] = state - (fars[slot] + 16.0 * update(2))

            return carry

        lax.fori_loop(0, slot_last, last_pass, 0)

    results = (
        pltpu.make_async_copy(states, out_states, store.at[0]),
        pltpu.make_async_copy(four, out_four, store.at[1]),
        pltpu.make_async_copy(sixteen, out_sixteen, store.at[2]),
    )
    for copy in results:
        copy.start()

    @pl.when(here < end)
    def _():
        give_relaxed.wait_send()
        for slot in range(slot_last):
            give_left(slot).wait_send()

    @pl.when(here == half - 1)
    def _():
        give_far_relaxed.wait_send()

    @pl.when((here >= half) & (here < end))
    def _():
        give_middle.wait_send()

    @pl.when((here > 0) & (here < end))
    def _():
        give_final.wait_send()

    @pl.when(here < half)
    def _():
        give_far_final.wait_send()
        for slot in range(slot_last):
            give_far(slot).wait_send()

    sums = summed[...]
    for k in range(1, sections):
        along_copy(k).wait()
        sums = sums + along[k - 1]
    ratios[...] = jnp.sqrt(sums[0:1] / (sums[1:2] + epsilon))
    for copy in results:
        copy.wait()


def cycle(initial, norm_gains, first_weights, second_weights):
    sections = lax.axis_size("layer")
    copies = lax.axis_size("dp")
    shape = initial.shape
    slot_count, width, ff = first_weights.shape
    rows = shape[0]
    anywhere = pl.BlockSpec(memory_space=pl.ANY)
    held = (slot_count,) + shape
    inner = (slot_count - 1,) + shape
    dma = pltpu.SemaphoreType.DMA

    def single(*dims):
        return pltpu.VMEM(dims, jnp.float32)

    states, four, sixteen, ratios = pl.pallas_call(
        lambda *refs: cycle_kernel(sections, copies, *refs),
        out_shape=(
            jax.ShapeDtypeStruct(held, jnp.float32),
            jax.ShapeDtypeStruct(held, jnp.float32),
            jax.ShapeDtypeStruct(held, jnp.float32),
            jax.ShapeDtypeStruct((1, 128), jnp.float32),
        ),
        in_specs=[anywhere] * 4,
        out_specs=(anywhere, anywhere, anywhere, pl.BlockSpec(memory_space=pltpu.VMEM)),
        scratch_shapes=[
            pltpu.VMEM(first_weights.shape, jnp.bfloat16),
            pltpu.VMEM(second_weights.shape, jnp.bfloat16),
            single(slot_count, width),
            single(*shape),
            pltpu.VMEM((3 * rows, width), jnp.bfloat16),
            pltpu.VMEM((3 * rows, ff), jnp.bfloat16),
            single(3 * rows, width),
            single(*shape),
            single(*shape), single(*shape), single(*shape), single(*shape), single(*shape),
            single(*shape), single(*shape), single(*shape), single(*shape), single(*shape),
            single(*inner), single(*inner),
            single(*held), single(*held), single(*held),
            single(8, 128), single(copies, 8, 128), single(sections - 1, 8, 128), single(8, 128),
            dma((slot_count,)), dma((slot_count,)), dma((2,)), dma((3,)),
            dma((5,)), dma((5,)), dma((2, slot_count - 1)), dma((2, slot_count - 1)),
            dma((copies - 1,)), dma((copies - 1,)),
            dma((sections - 1,)), dma((sections - 1,)),
        ],
        compiler_params=pltpu.CompilerParams(
            collective_id=0, has_side_effects=True, vmem_limit_bytes=60 * 1024 * 1024
        ),
        name="cycle",
    )(initial, norm_gains, first_weights, second_weights)
    return (states, ratios[0, : sections - 1], four, sixteen)


def chosen(initial, norm_gains, first_weights, second_weights):
    sections = lax.axis_size("layer")
    fits = first_weights.shape[0] == 4 and sections == 8 and lax.axis_size("dp") > 1
    return (cycle if fits else local)(initial, norm_gains, first_weights, second_weights)


def solution(mesh):
    placed = (P("dp", None), P("layer", None), P("layer", None, None), P("layer", None, None))
    return jax.shard_map(
        chosen,
        mesh=mesh,
        in_specs=placed,
        out_specs=(P("layer", "dp", None), P(), P("layer", "dp", None), P("layer", "dp", None)),
        check_vma=False,
    )
```

time: 185 us -> 78.7 us (0.43)
  the two profiles are of different devices: /device:TPU:0 before, /device:TPU:31 now
where the time goes in v1:
time: 78.7 us; the launch traced here: 78.5 us
  Pallas kernels  69.8 us (89%)
  local copies, waits for them, and re-layouts  8.04 us (10%)
    pallas_call x1, Pallas kernels, cycle(): pl.pallas_call(lambda *refs: cycle_kernel(sections, copies, *refs), out_s...  69.8 us
    unnamed x3, local copies, waits for them, and re-layouts  6.92 us

profile of v1, /device:TPU:31, one launch (start us, length us, event | category | flops | bytes accessed | tf_op | source)
XLA Modules:
  0.0 78.5 jit_solution(13134392588758795353)
XLA Ops:
  0.6 69.8 %cycle.1 = (f32[4,64,1024]{2,1,0:T(8,128)}, f32[4,64,1024]{2,1,0:T(8,128)}, f32[4,64,1024]{2,1,0:T(8,128)}, f32[1,128]{1,0:T(1,128)}) custom-call(f32[64,1024]{1,0:T(8,128)} %refs_0_.1, f32[4,1024]{1,0:T(4,128)} %refs_1_.1, bf16[4,1024,2048]{2,1,0:T(8,128)(2,1)} %refs_2_.1, bf16[4,2048,1024]{2,1,0:T(8,128)(2,1)} %refs_3_.1), custom_call_target="tpu_custom_call" | custom-call | tf_op jit(solution)/shard_map/cycle/pallas_call | solution.py:591
  70.4 1.1 %slice_bitcast_fusion = f32[7]{0:T(128)} fusion(f32[1,128]{1,0:T(1,128)} %get-tuple-element.9), kind=kLoop, calls=%fused_computation | loop fusion | bytes 56 | tf_op jit(solution)/shard_map/squeeze | solution.py:625
  71.5 2.3 %copy.11 = f32[4,64,1024]{2,1,0:T(8,128)} copy(f32[4,64,1024]{2,1,0:T(8,128)} %get-tuple-element.16) | data formatting | bytes 2097152
  73.8 2.3 %copy.12 = f32[4,64,1024]{2,1,0:T(8,128)} copy(f32[4,64,1024]{2,1,0:T(8,128)} %get-tuple-element.18) | data formatting | bytes 2097152
  76.2 2.3 %copy.13 = f32[4,64,1024]{2,1,0:T(8,128)} copy(f32[4,64,1024]{2,1,0:T(8,128)} %get-tuple-element.19) | data formatting | bytes 2097152

commit v2 on v1

--- a/solution.py
+++ b/solution.py
@@ -190,12 +190,12 @@
 def cycle_kernel(
     sections, copies,
     initial, norm_gains, first_weights, second_weights,
-    out_states, out_four, out_sixteen, ratios,
+    states, four, sixteen, ratios,
     w_in, w_out, gain, start, normed, hidden, total, cur,
     relaxed, middle, final, rhs, wide_start,
-    left_relaxed, left_middle, left_final, far_relaxed, far_final, lefts, fars,
-    states, four, sixteen, tile, across, along, summed,
-    load_in, load_out, load_small, store,
+    fine, near, left_relaxed, left_middle, left_final, far_relaxed, far_final, lefts, fars,
+    tile, across, along, summed,
+    load_in, load_out, load_small,
     send_point, take_point, send_state, take_state,
     across_send, across_take, along_send, along_take,
 ):
@@ -220,7 +220,8 @@
     load_gain = pltpu.make_async_copy(norm_gains, gain, load_small.at[1])
     load_start.start()
     load_gain.start()
-    for slot in range(slot_count):
+    ahead = min(2, slot_count)
+    for slot in range(ahead):
         load_first(slot).start()
         load_second(slot).start()
 
@@ -308,8 +309,18 @@
         normalise(0, cur[...], slot)
         normalise(1, start[...], slot)
         load_first(slot).wait()
+
+        @pl.when(slot + ahead < slot_count)
+        def _():
+            load_first(slot + ahead).start()
+
         project_in(2, slot)
         load_second(slot).wait()
+
+        @pl.when(slot + ahead < slot_count)
+        def _():
+            load_second(slot + ahead).start()
+
         project_out(2, slot)
         state = cur[...] + update(0)
         cur[...] = state
@@ -328,10 +339,6 @@
     def _():
         give_far_relaxed.start()
 
-    four[...] = jnp.zeros_like(four)
-    sixteen[...] = jnp.zeros_like(sixteen)
-    tile[...] = jnp.zeros_like(tile)
-
     @pl.when(here == half - 1)
     def _():
         wide_start[...] = start[...] + 16.0 * update(1)
@@ -340,10 +347,12 @@
     def _():
         final[...] = relaxed[...]
         give_far_final.start()
-        four[slot_last] = relaxed[...] - (start[...] + 4.0 * update(1))
         for slot in range(slot_last):
             give_left(slot).start()
             give_far(slot).start()
+            four[slot] = jnp.zeros_like(start)
+        four[slot_last] = relaxed[...] - (start[...] + 4.0 * update(1))
+        tile[...] = jnp.zeros_like(tile)
 
     @pl.when(here > 0)
     def _():
@@ -380,26 +389,25 @@
             middle[...] = cur[...]
             give_middle.start()
 
-        fine = cur[...]
-        source = fine - (left_relaxed[...] + 4.0 * update(1))
+        point = cur[...]
+        source = point - (left_relaxed[...] + 4.0 * update(1))
         rhs[...] = source
+        fine[...] = point
+        near[...] = update(0)
 
         @pl.when(here == 1)
         def _():
             four[slot_last] = source
 
-        gap = fine - relaxed[...]
-        near_term = update(0)
+    def take_sums():
+        gap = fine[...] - relaxed[...]
+        near_term = near[...]
         lane = lax.broadcasted_iota(jnp.int32, tile.shape, 1) == here - 1
         row = lax.broadcasted_iota(jnp.int32, tile.shape, 0)
         tile[...] = jnp.where(lane & (row == 0), jnp.sum(gap * gap), 0.0) + jnp.where(
             lane & (row == 1), jnp.sum(near_term * near_term), 0.0
         )
 
-    across[depth] = tile[...]
-    for k in range(1, copies):
-        across_copy(k).start()
-
     def coarse_pass(r, carry):
         middle_round = (r == 0) & (here > half)
         wide_round = (r == 1) & (here == end)
@@ -471,9 +479,61 @@
                 def _():
                     sixteen[slot_last] = point - (far_final[...] + 16.0 * update(1))
 
+        @pl.when(r == 0)
+        def _():
+            @pl.when(here > 0)
+            def _():
+                take_sums()
+
+            across[depth] = tile[...]
+            for k in range(1, copies):
+                across_copy(k).start()
+
         return carry
 
     lax.fori_loop(0, 3, coarse_pass, 0)
+
+    states[slot_last] = final[...]
+
+    def advance(slot):
+        state = cur[...] + update(0)
+        cur[...] = state
+        states[slot] = state
+
+        @pl.when(here < end)
+        def _():
+            give_left(slot).start()
+
+        @pl.when(here < half)
+        def _():
+            give_far(slot).start()
+
+    def take_left(slot, part):
+        give_left(slot).wait_recv()
+        normalise(part, lefts[slot], slot)
+
+    def take_far(slot, part):
+        give_far(slot).wait_recv()
+        normalise(part, fars[slot], slot)
+
+    def defect_four(slot, part):
+        four[slot] = states[slot] - (lefts[slot] + 4.0 * update(part))
+
+    def defect_sixteen(slot, part):
+        sixteen[slot] = states[slot] - (fars[slot] + 16.0 * update(part))
+
+    @pl.when((here > 1) & (here < end))
+    def _():
+        cur[...] = left_final[...]
+
+        def state_pass(slot, carry):
+            normalise(0, cur[...], slot)
+            project_in(2, slot)
+            project_out(2, slot)
+            advance(slot)
+            return carry
+
+        lax.fori_loop(0, slot_last, state_pass, 0)
 
     for k in range(1, copies):
         across_copy(k).wait()
@@ -484,62 +544,54 @@
     for k in range(1, sections):
         along_copy(k).start()
 
-    states[slot_last] = final[...]
-
-    @pl.when(here > 0)
-    def _():
-        @pl.when(here > 1)
-        def _():
-            cur[...] = left_final[...]
+    @pl.when((here > 0) & (here < end))
+    def _():
+        def defect_pass(slot, carry):
+            take_left(slot, 0)
+
+            @pl.when(here >= half)
+            def _():
+                take_far(slot, 1)
+
+            project_in(2, slot)
+            project_out(2, slot)
+            defect_four(slot, 0)
+
+            @pl.when(here >= half)
+            def _():
+                defect_sixteen(slot, 1)
+
+            return carry
+
+        lax.fori_loop(0, slot_last, defect_pass, 0)
+
+    @pl.when(here == end)
+    def _():
+        cur[...] = left_final[...]
 
         def last_pass(slot, carry):
-            @pl.when(here > 1)
-            def _():
-                normalise(0, cur[...], slot)
-
-            give_left(slot).wait_recv()
-            normalise(1, lefts[slot], slot)
-
-            @pl.when(here >= half)
-            def _():
-                give_far(slot).wait_recv()
-                normalise(2, fars[slot], slot)
-
+            normalise(0, cur[...], slot)
+            take_far(slot, 2)
+            take_left(slot, 1)
             project_in(3, slot)
             project_out(3, slot)
-
-            @pl.when(here > 1)
-            def _():
-                state = cur[...] + update(0)
-                cur[...] = state
-                states[slot] = state
-
-                @pl.when(here < end)
-                def _():
-                    give_left(slot).start()
-
-                @pl.when(here < half)
-                def _():
-                    give_far(slot).start()
-
-            state = states[slot]
-            four[slot] = state - (lefts[slot] + 4.0 * update(1))
-
-            @pl.when(here >= half)
-            def _():
-                sixteen[slot] = state - (fars[slot] + 16.0 * update(2))
-
+            state = cur[...] + update(0)
+            cur[...] = state
+            states[slot] = state
+            defect_four(slot, 1)
+            defect_sixteen(slot, 2)
             return carry
 
         lax.fori_loop(0, slot_last, last_pass, 0)
 
-    results = (
-        pltpu.make_async_copy(states, out_states, store.at[0]),
-        pltpu.make_async_copy(four, out_four, store.at[1]),
-        pltpu.make_async_copy(sixteen, out_sixteen, store.at[2]),
-    )
-    for copy in results:
-        copy.start()
+    @pl.when(here < half)
+    def _():
+        for slot in range(slot_last):
+            sixteen[slot] = jnp.zeros_like(start)
+
+    @pl.when(here < half - 1)
+    def _():
+        sixteen[slot_last] = jnp.zeros_like(start)
 
     @pl.when(here < end)
     def _():
@@ -570,7 +622,17 @@
         along_copy(k).wait()
         sums = sums + along[k - 1]
     ratios[...] = jnp.sqrt(sums[0:1] / (sums[1:2] + epsilon))
-    for copy in results:
+
+
+def finish_kernel(states, ratios, four, sixteen, out_states, out_ratios, out_four, out_sixteen, store):
+    pairs = ((states, out_states), (four, out_four), (sixteen, out_sixteen))
+    copies = [
+        pltpu.make_async_copy(held, out, store.at[i]) for i, (held, out) in enumerate(pairs)
+    ]
+    for copy in copies:
+        copy.start()
+    out_ratios[...] = ratios[0, : out_ratios.shape[0]]
+    for copy in copies:
         copy.wait()
 
 
@@ -581,6 +643,7 @@
     slot_count, width, ff = first_weights.shape
     rows = shape[0]
     anywhere = pl.BlockSpec(memory_space=pl.ANY)
+    inside = pl.BlockSpec(memory_space=pltpu.VMEM)
     held = (slot_count,) + shape
     inner = (slot_count - 1,) + shape
     dma = pltpu.SemaphoreType.DMA
@@ -591,13 +654,13 @@
     states, four, sixteen, ratios = pl.pallas_call(
         lambda *refs: cycle_kernel(sections, copies, *refs),
         out_shape=(
-            jax.ShapeDtypeStruct(held, jnp.float32),
-            jax.ShapeDtypeStruct(held, jnp.float32),
-            jax.ShapeDtypeStruct(held, jnp.float32),
-            jax.ShapeDtypeStruct((1, 128), jnp.float32),
+            pltpu.VMEM(held, jnp.float32),
+            pltpu.VMEM(held, jnp.float32),
+            pltpu.VMEM(held, jnp.float32),
+            pltpu.VMEM((1, 128), jnp.float32),
         ),
-        in_specs=[anywhere] * 4,
-        out_specs=(anywhere, anywhere, anywhere, pl.BlockSpec(memory_space=pltpu.VMEM)),
+        in_specs=[pl.BlockSpec(memory_space=pltpu.HBM)] * 4,
+        out_specs=(inside,) * 4,
         scratch_shapes=[
             pltpu.VMEM(first_weights.shape, jnp.bfloat16),
             pltpu.VMEM(second_weights.shape, jnp.bfloat16),
@@ -607,22 +670,35 @@
             pltpu.VMEM((3 * rows, ff), jnp.bfloat16),
             single(3 * rows, width),
             single(*shape),
-            single(*shape), single(*shape), single(*shape), single(*shape), single(*shape),
-            single(*shape), single(*shape), single(*shape), single(*shape), single(*shape),
+            single(*shape), single(*shape), single(*shape), single(*shape), single(*shape), single(*shape),
+            single(*shape), single(*shape), single(*shape), single(*shape), single(*shape), single(*shape),
             single(*inner), single(*inner),
-            single(*held), single(*held), single(*held),
             single(8, 128), single(copies, 8, 128), single(sections - 1, 8, 128), single(8, 128),
-            dma((slot_count,)), dma((slot_count,)), dma((2,)), dma((3,)),
+            dma((slot_count,)), dma((slot_count,)), dma((2,)),
             dma((5,)), dma((5,)), dma((2, slot_count - 1)), dma((2, slot_count - 1)),
             dma((copies - 1,)), dma((copies - 1,)),
             dma((sections - 1,)), dma((sections - 1,)),
         ],
         compiler_params=pltpu.CompilerParams(
-            collective_id=0, has_side_effects=True, vmem_limit_bytes=60 * 1024 * 1024
+            collective_id=0, has_side_effects=True, vmem_limit_bytes=62384 * 1024
         ),
         name="cycle",
     )(initial, norm_gains, first_weights, second_weights)
-    return (states, ratios[0, : sections - 1], four, sixteen)
+    out_states, out_ratios, out_four, out_sixteen = pl.pallas_call(
+        finish_kernel,
+        out_shape=(
+            jax.ShapeDtypeStruct(held, jnp.float32),
+            jax.ShapeDtypeStruct((sections - 1,), jnp.float32),
+            jax.ShapeDtypeStruct(held, jnp.float32),
+            jax.ShapeDtypeStruct(held, jnp.float32),
+        ),
+        in_specs=[inside] * 4,
+        out_specs=(anywhere, inside, anywhere, anywhere),
+        scratch_shapes=[dma((3,))],
+        compiler_params=pltpu.CompilerParams(vmem_limit_bytes=8 * 1024 * 1024),
+        name="finish",
+    )(states, ratios, four, sixteen)
+    return (out_states, out_ratios, out_four, out_sixteen)
 
 
 def chosen(initial, norm_gains, first_weights, second_weights):

time: 78.7 us -> 59.5 us (0.76)
  Pallas kernels: 69.8 us -> 58.7 us
  local copies, waits for them, and re-layouts: 8.04 us -> 0 us
    pallas_call x1, Pallas kernels: 69.8 us -> 56.5 us  [cycle(): pl.pallas_call(lambda *refs: cycle_kernel(sections, copies, *refs), out_s...]
    unnamed x3 -> x0, local copies, waits for them, and re-layouts: 6.92 us -> none
    pallas_call x0 -> x1, Pallas kernels: none -> 2.2 us  [cycle(): pl.pallas_call(finish_kernel, out_shape=(jax.ShapeDtypeStruct(held, jnp.f...]
    squeeze x1 -> x0, local copies, waits for them, and re-layouts: 1.12 us -> none  [cycle(): return (states, ratios[0, :sections - 1], four, sixteen)]
where the time goes in v2:
time: 59.5 us; the launch traced here: 59.3 us
  Pallas kernels  58.7 us (99%)
  between operations  0.64 us (1%)
    pallas_call x1, Pallas kernels, cycle(): pl.pallas_call(lambda *refs: cycle_kernel(sections, copies, *refs), out_s...  56.5 us
    pallas_call x1, Pallas kernels, cycle(): pl.pallas_call(finish_kernel, out_shape=(jax.ShapeDtypeStruct(held, jnp.f...  2.2 us

profile of v2, /device:TPU:31, one launch (start us, length us, event | category | flops | bytes accessed | tf_op | source)
XLA Modules:
  0.0 59.3 jit_solution(10672405919165867247)
XLA Ops:
  0.6 56.5 %cycle.1 = (f32[4,64,1024]{2,1,0:T(8,128)S(1)}, f32[4,64,1024]{2,1,0:T(8,128)S(1)}, f32[4,64,1024]{2,1,0:T(8,128)S(1)}, f32[1,128]{1,0:T(1,128)S(1)}) custom-call(f32[64,1024]{1,0:T(8,128)} %refs_0_.1, f32[4,1024]{1,0:T(4,128)} %refs_1_.1, bf16[4,1024,2048]{2,1,0:T(8,128)(2,1)} %refs_2_.1, bf16[4,2048,1024]{2,1,0:T(8,128)(2,1)} %refs_3_.1), custom_call_target="tpu_custom_call" | custom-call | tf_op jit(solution)/shard_map/cycle/pallas_call | solution.py:654
  57.1 2.2 %finish.1 = (f32[4,64,1024]{2,1,0:T(8,128)}, f32[7]{0:T(128)}, f32[4,64,1024]{2,1,0:T(8,128)}, f32[4,64,1024]{2,1,0:T(8,128)}) custom-call(f32[4,64,1024]{2,1,0:T(8,128)S(1)} %get-tuple-element.8.states, f32[1,128]{1,0:T(1,128)S(1)} %get-tuple-element.9.ratios, f32[4,64,1024]{2,1,0:T(8,128)S(1)} %get-tuple-element.10.four, ...), custom_call_target="tpu_custom_call" | custom-call | tf_op jit(solution)/shard_map/finish/pallas_call | solution.py:687

commit v3 on v2

--- a/solution.py
+++ b/solution.py
@@ -194,7 +194,7 @@
     w_in, w_out, gain, start, normed, hidden, total, cur,
     relaxed, middle, final, rhs, wide_start,
     fine, near, left_relaxed, left_middle, left_final, far_relaxed, far_final, lefts, fars,
-    tile, across, along, summed,
+    scale, partial, tile, across, along, summed,
     load_in, load_out, load_small,
     send_point, take_point, send_state, take_state,
     across_send, across_take, along_send, along_take,
@@ -240,9 +240,16 @@
 
     give_relaxed = point_send(0, relaxed, left_relaxed, 1)
     give_far_relaxed = point_send(1, relaxed, far_relaxed, half)
-    give_middle = point_send(2, middle, left_middle, 1)
-    give_final = point_send(3, final, left_final, 1)
-    give_far_final = point_send(4, final, far_final, half)
+    give_far_final = point_send(2, final, far_final, half)
+    parts_of_row = [pl.ds(i * width // 2, width // 2) for i in range(2)]
+    give_middle = [
+        point_send(3 + i, middle.at[:, cols], left_middle.at[:, cols], 1)
+        for i, cols in enumerate(parts_of_row)
+    ]
+    give_final = [
+        point_send(5 + i, final.at[:, cols], left_final.at[:, cols], 1)
+        for i, cols in enumerate(parts_of_row)
+    ]
 
     def state_send(slot, target, distance, row):
         return pltpu.make_async_remote_copy(
@@ -378,7 +385,8 @@
         @pl.when(here == 1)
         def _():
             final[...] = cur[...]
-            give_final.start()
+            for copy in give_final:
+                copy.start()
             give_far_final.start()
             for slot in range(slot_last):
                 give_left(slot).start()
@@ -387,7 +395,8 @@
         @pl.when(here == half)
         def _():
             middle[...] = cur[...]
-            give_middle.start()
+            for copy in give_middle:
+                copy.start()
 
         point = cur[...]
         source = point - (left_relaxed[...] + 4.0 * update(1))
@@ -408,6 +417,59 @@
             lane & (row == 1), jnp.sum(near_term * near_term), 0.0
         )
 
+    halves = [slice(i * width // 2, (i + 1) * width // 2) for i in range(2)]
+
+    def weigh(part, source):
+        values = source[...]
+        span = slice(part * rows, (part + 1) * rows)
+        mean_square = jnp.mean(values * values, axis=-1, keepdims=True)
+        normed[span, :] = (values * gain[slot_last : slot_last + 1, :]).astype(jnp.bfloat16)
+        scale[span, :] = jnp.broadcast_to(lax.rsqrt(mean_square + epsilon), (rows, 128))
+
+    def weigh_half(i, source):
+        cols = halves[i]
+        values = source[:, cols]
+        squares = jnp.sum(values * values, axis=-1, keepdims=True)
+        normed[:rows, cols] = (values * gain[slot_last : slot_last + 1, cols]).astype(jnp.bfloat16)
+        if i == 0:
+            scale[:rows, :] = jnp.broadcast_to(squares, (rows, 128))
+        else:
+            scale[:rows, :] = lax.rsqrt((scale[:rows, :] + squares) * (1.0 / width) + epsilon)
+
+    def project_half(i):
+        step = ff // 4
+        for j in range(4):
+            cols = slice(j * step, (j + 1) * step)
+            product = jnp.dot(
+                normed[: 2 * rows, halves[i]], w_in[slot_last, halves[i], cols],
+                preferred_element_type=jnp.float32,
+            )
+            if i == 0:
+                partial[:, cols] = product
+            else:
+                hidden[: 2 * rows, cols] = jax.nn.gelu(
+                    (partial[:, cols] + product) * scale[:, 0:1], approximate=True
+                ).astype(jnp.bfloat16)
+
+    def project_out_half(i):
+        step = width // 4
+        for j in (2 * i, 2 * i + 1):
+            cols = slice(j * step, (j + 1) * step)
+            total[: 2 * rows, cols] = jnp.dot(
+                hidden[: 2 * rows, :], w_out[slot_last, :, cols],
+                preferred_element_type=jnp.float32,
+            )
+
+    def exchange():
+        for k in range(1, copies):
+            across_copy(k).wait()
+        gathered = across[0]
+        for k in range(1, copies):
+            gathered = gathered + across[k]
+        summed[...] = gathered
+        for k in range(1, sections):
+            along_copy(k).start()
+
     def coarse_pass(r, carry):
         middle_round = (r == 0) & (here > half)
         wide_round = (r == 1) & (here == end)
@@ -415,38 +477,50 @@
 
         @pl.when(middle_round | wide_round | final_round)
         def _():
-            @pl.when(middle_round)
-            def _():
-                give_middle.wait_recv()
-                normalise(0, left_middle[...], slot_last)
-
             @pl.when(wide_round)
             def _():
                 give_far_relaxed.wait_recv()
-                normalise(1, far_relaxed[...], slot_last)
+                weigh(1, far_relaxed)
                 give_far_final.wait_recv()
-                normalise(0, far_final[...], slot_last)
-
-            @pl.when(final_round)
+
+            @pl.when(final_round & (here >= half) & (here < end))
             def _():
-                @pl.when((here >= half) & (here < end))
-                def _():
-                    give_far_final.wait_recv()
-                    normalise(1, far_final[...], slot_last)
-
-                give_final.wait_recv()
-                normalise(0, left_final[...], slot_last)
-
-            project_in(2, slot_last)
-            project_out(2, slot_last)
-
-            @pl.when(middle_round)
-            def _():
-                middle[...] = left_middle[...] + 4.0 * update(0) + rhs[...]
-
-                @pl.when(here < end)
-                def _():
-                    give_middle.start()
+                give_far_final.wait_recv()
+                weigh(1, far_final)
+
+            for i in range(2):
+                @pl.when(middle_round)
+                def _(i=i):
+                    give_middle[i].wait_recv()
+                    weigh_half(i, left_middle)
+
+                @pl.when(wide_round)
+                def _(i=i):
+                    weigh_half(i, far_final)
+
+                @pl.when(final_round)
+                def _(i=i):
+                    give_final[i].wait_recv()
+                    weigh_half(i, left_final)
+
+                project_half(i)
+
+            for i in range(2):
+                project_out_half(i)
+                cols = halves[i]
+
+                @pl.when(middle_round)
+                def _(i=i, cols=cols):
+                    middle[:, cols] = left_middle[:, cols] + 4.0 * total[:rows, cols] + rhs[:, cols]
+
+                    @pl.when(here < end)
+                    def _():
+                        give_middle[i].start()
+
+                @pl.when(final_round & (here < end))
+                def _(i=i, cols=cols):
+                    final[:, cols] = left_final[:, cols] + 4.0 * total[:rows, cols] + rhs[:, cols]
+                    give_final[i].start()
 
             @pl.when(wide_round)
             def _():
@@ -457,19 +531,12 @@
 
             @pl.when(final_round)
             def _():
-                stepped = left_final[...] + 4.0 * update(0)
-
-                @pl.when(here < end)
-                def _():
-                    final[...] = stepped + rhs[...]
-                    give_final.start()
-
                 @pl.when(here < half)
                 def _():
                     give_far_final.start()
 
                 point = final[...]
-                four[slot_last] = point - stepped
+                four[slot_last] = point - (left_final[...] + 4.0 * update(0))
 
                 @pl.when(here == half - 1)
                 def _():
@@ -488,6 +555,10 @@
             across[depth] = tile[...]
             for k in range(1, copies):
                 across_copy(k).start()
+
+        @pl.when((r == 1) & ((here < 2) | (here >= half)))
+        def _():
+            exchange()
 
         return carry
 
@@ -535,14 +606,9 @@
 
         lax.fori_loop(0, slot_last, state_pass, 0)
 
-    for k in range(1, copies):
-        across_copy(k).wait()
-    gathered = across[0]
-    for k in range(1, copies):
-        gathered = gathered + across[k]
-    summed[...] = gathered
-    for k in range(1, sections):
-        along_copy(k).start()
+    @pl.when((here > 1) & (here < half))
+    def _():
+        exchange()
 
     @pl.when((here > 0) & (here < end))
     def _():
@@ -605,11 +671,13 @@
 
     @pl.when((here >= half) & (here < end))
     def _():
-        give_middle.wait_send()
+        for copy in give_middle:
+            copy.wait_send()
 
     @pl.when((here > 0) & (here < end))
     def _():
-        give_final.wait_send()
+        for copy in give_final:
+            copy.wait_send()
 
     @pl.when(here < half)
     def _():
@@ -673,9 +741,10 @@
             single(*shape), single(*shape), single(*shape), single(*shape), single(*shape), single(*shape),
             single(*shape), single(*shape), single(*shape), single(*shape), single(*shape), single(*shape),
             single(*inner), single(*inner),
+            single(2 * rows, 128), single(2 * rows, ff),
             single(8, 128), single(copies, 8, 128), single(sections - 1, 8, 128), single(8, 128),
             dma((slot_count,)), dma((slot_count,)), dma((2,)),
-            dma((5,)), dma((5,)), dma((2, slot_count - 1)), dma((2, slot_count - 1)),
+            dma((7,)), dma((7,)), dma((2, slot_count - 1)), dma((2, slot_count - 1)),
             dma((copies - 1,)), dma((copies - 1,)),
             dma((sections - 1,)), dma((sections - 1,)),
         ],

time: 59.5 us -> 57 us (0.958)
  Pallas kernels: 58.7 us -> 56.2 us
    pallas_call x1, Pallas kernels: 56.5 us -> 54 us  [cycle(): pl.pallas_call(lambda *refs: cycle_kernel(sections, copies, *refs), out_s...]
where the time goes in v3:
time: 57 us; the launch traced here: 56.8 us
  Pallas kernels  56.2 us (99%)
  between operations  0.64 us (1%)
    pallas_call x1, Pallas kernels, cycle(): pl.pallas_call(lambda *refs: cycle_kernel(sections, copies, *refs), out_s...  54 us
    pallas_call x1, Pallas kernels, cycle(): pl.pallas_call(finish_kernel, out_shape=(jax.ShapeDtypeStruct(held, jnp.f...  2.2 us

profile of v3, /device:TPU:31, one launch (start us, length us, event | category | flops | bytes accessed | tf_op | source)
XLA Modules:
  0.0 56.8 jit_solution(415035259647427778)
XLA Ops:
  0.6 54.0 %cycle.1 = (f32[4,64,1024]{2,1,0:T(8,128)S(1)}, f32[4,64,1024]{2,1,0:T(8,128)S(1)}, f32[4,64,1024]{2,1,0:T(8,128)S(1)}, f32[1,128]{1,0:T(1,128)S(1)}) custom-call(f32[64,1024]{1,0:T(8,128)} %refs_0_.1, f32[4,1024]{1,0:T(4,128)} %refs_1_.1, bf16[4,1024,2048]{2,1,0:T(8,128)(2,1)} %refs_2_.1, bf16[4,2048,1024]{2,1,0:T(8,128)(2,1)} %refs_3_.1), custom_call_target="tpu_custom_call" | custom-call | tf_op jit(solution)/shard_map/cycle/pallas_call | solution.py:722
  54.6 2.2 %finish.1 = (f32[4,64,1024]{2,1,0:T(8,128)}, f32[7]{0:T(128)}, f32[4,64,1024]{2,1,0:T(8,128)}, f32[4,64,1024]{2,1,0:T(8,128)}) custom-call(f32[4,64,1024]{2,1,0:T(8,128)S(1)} %get-tuple-element.8.states, f32[1,128]{1,0:T(1,128)S(1)} %get-tuple-element.9.ratios, f32[4,64,1024]{2,1,0:T(8,128)S(1)} %get-tuple-element.10.four, ...), custom_call_target="tpu_custom_call" | custom-call | tf_op jit(solution)/shard_map/finish/pallas_call | solution.py:756
